TPU v7x, 32 devices: a whole 2x2x4 slice. The times are simulated.
32 devices in a mesh: row: 8 (over z, x), col: 4 (over y, core).
Axes of the slice: x: 2, y: 2, z: 4, core: 2. Of those that a mesh axis runs over, the one named last changes fastest.
Arguments:
- normal_matrix: float32 [9216, 9216], P('row', 'col'), may hold values from -1 to 6, as said below
- right_side: float32 [9216, 64], P('col'), may hold values from -6 to 6
- tile_inverse: float32 [72, 128, 128], P('col'), may hold values from -1 to 3.5, as said below
- order_ids: int32 [9216], P('col'), may hold values from 0 to 96, never falling along the last dimension, each value on 1 to 194 neighbouring positions
Outputs:
- solution: float32 [9216, 64], P('col')
- residual: float32 [9216, 64], P('col')
Inputs may be any that keep to these rules, and one draw needn't show every extreme that they name: `normal_matrix`: symmetric and positive definite. `tile_inverse`: each tile symmetric, every principal submatrix of it positive definite. `order_ids`: never falling along the coefficients; each order holds 1 to 194 coefficients.
All inputs are finite; a program needn't handle non-finite values.
Results may differ from a plain program's by a relative error of at most 0.0003.
Values sent between devices are 32-bit elements; how exact they have to be, the bound alone decides.
A program may use at most 64 MiB of HBM per device.

v0:
```python
import functools

import jax
import jax.numpy as jnp
from jax import lax
from jax.experimental import pallas as pl
from jax.experimental.pallas import tpu as pltpu
from jax.sharding import PartitionSpec as P

ITERS = 2
MESH = pl.DeviceIdType.MESH
CHUNKS = 9
LAGS = (0, 2, 6, 8)


def masked_tiles(tile_inverse, order_ids):
    count = tile_inverse.shape[0]
    width = tile_inverse.shape[1]
    order_tile = order_ids.reshape(count, width)
    same_order = order_tile[:, :, None] == order_tile[:, None, :]
    return jnp.where(same_order, tile_inverse, jnp.float32(0.0))


def apply_precond(tile_inverse, order_ids, vector):
    count = tile_inverse.shape[0]
    width = tile_inverse.shape[1]
    masked = masked_tiles(tile_inverse, order_ids)
    pieces = vector.reshape(count, width, vector.shape[1])
    result = jnp.einsum("tij,tjk->tik", masked, pieces, precision=lax.Precision.HIGHEST)
    return result.reshape(vector.shape)


def plain_body(normal_matrix, right_side, tile_inverse, order_ids):
    block_rows = normal_matrix.shape[0]

    def apply_matrix(vector):
        first_row = lax.axis_index("row") * block_rows
        gathered = lax.all_gather(vector, "col", axis=0, tiled=True)
        row_piece = lax.dynamic_slice_in_dim(gathered, first_row, block_rows, 0)
        partial_value = lax.dot_general(
            normal_matrix,
            row_piece,
            (((0,), (0,)), ((), ())),
            precision=lax.Precision.HIGHEST,
            preferred_element_type=jnp.float32,
        )
        return lax.psum(partial_value, "row")

    solution = jnp.zeros_like(right_side)
    residual = right_side
    precond_res = apply_precond(tile_inverse, order_ids, residual)
    image_res = apply_matrix(precond_res)
    image_dir = jnp.zeros_like(right_side)
    precond_dir = jnp.zeros_like(right_side)
    residual_dir = jnp.zeros_like(right_side)
    direction = jnp.zeros_like(right_side)
    gamma_prev = jnp.ones((right_side.shape[1],), jnp.float32)
    alpha_prev = jnp.ones((right_side.shape[1],), jnp.float32)
    for iteration in range(ITERS):
        gamma_now, delta_now = lax.psum(
            (jnp.sum(residual * precond_res, axis=0), jnp.sum(image_res * precond_res, axis=0)),
            "col",
        )
        precond_img = apply_precond(tile_inverse, order_ids, image_res)
        image_img = apply_matrix(precond_img)
        if iteration == 0:
            beta_ratio = jnp.zeros_like(gamma_now)
            step_size = gamma_now / delta_now
        else:
            beta_ratio = gamma_now / gamma_prev
            step_size = gamma_now / (delta_now - beta_ratio * gamma_now / alpha_prev)
        image_dir = image_img + beta_ratio * image_dir
        precond_dir = precond_img + beta_ratio * precond_dir
        residual_dir = image_res + beta_ratio * residual_dir
        direction = precond_res + beta_ratio * direction
        solution = solution + step_size * direction
        residual = residual - step_size * residual_dir
        precond_res = precond_res - step_size * precond_dir
        image_res = image_res - step_size * image_dir
        gamma_prev = gamma_now
        alpha_prev = step_size
    return (solution, residual)


def split(value):
    high = value.astype(jnp.bfloat16)
    low = (value - high.astype(jnp.float32)).astype(jnp.bfloat16)
    return jnp.concatenate([high, low], axis=0)


def times_transposed(left, right):
    return lax.dot_general(
        left, right, (((1,), (1,)), ((), ())), preferred_element_type=jnp.float32
    )


def fold(product, rows, columns):
    upper = product[:rows, :columns] + product[rows:, :columns]
    lower = product[:rows, columns:] + product[rows:, columns:]
    return upper + lower


def kernel(
    row_count, group, chunks, width,
    a_ref, tile_ref, b_ref, ids_ref,
    sol_ref, res_ref,
    a_buf, a_split, tile_split, v_split, u_buf, m_buf,
    part, near, half, far, full, image,
    dot_own, dot_in, sums, i_buf, ids_buf,
    a_sem, near_sem, far_sem, full_sem, line_recv, line_send, side_recv, side_send, dot_send, dot_recv,
):
    my_row, my_col = lax.axis_index("row"), lax.axis_index("col")
    depth = row_count // group
    place, lane = my_row // group, lax.rem(my_row, group)
    core = lax.rem(my_col, 2)
    partner = my_col + 1 - 2 * core
    across = lax.rem(my_col + 2, 4)
    nrhs, block_cols = b_ref.shape
    block_rows = a_ref.shape[0]
    hh = nrhs // 2
    tiles = block_cols // width
    steps = block_rows // width
    piece = block_rows // chunks

    def fetch(i):
        rows = pl.ds(pl.multiple_of(i * width, width), width)
        return pltpu.make_async_copy(a_ref.at[rows], a_buf.at[i], a_sem.at[i])

    @pl.loop(0, steps)
    def _(i):
        fetch(i).start()

    barrier = pltpu.get_barrier_semaphore()
    for shift in range(1, 4):
        pl.semaphore_signal(
            barrier, inc=1, device_id=(my_row, lax.rem(my_col + shift, 4)), device_id_type=MESH
        )
    for shift in range(1, group):
        side = place * group + lax.rem(lane + shift, group)
        pl.semaphore_signal(barrier, inc=1, device_id=(side, my_col), device_id_type=MESH)

    @pl.when(place > 0)
    def _():
        pl.semaphore_signal(barrier, inc=1, device_id=(my_row - group, my_col), device_id_type=MESH)

    @pl.when(place < depth - 1)
    def _():
        pl.semaphore_signal(barrier, inc=1, device_id=(my_row + group, my_col), device_id_type=MESH)

    def tile_lanes(t):
        return pl.ds(pl.multiple_of(t * width, width), width)

    def precondition_tile(t, value, target):
        lanes = tile_lanes(t)
        value = fold(times_transposed(split(value), tile_split[t]), nrhs, width)
        target[:, lanes] = value
        v_split[:, lanes] = split(value)

    ids_buf[...] = jnp.zeros_like(ids_buf)
    ids_buf[0:tiles] = ids_ref[...].astype(jnp.float32)
    ids_across = ids_buf[...].T
    for t in range(tiles):
        same = ids_across[:, t : t + 1] == ids_buf[t : t + 1]
        tile_split[t] = split(jnp.where(same, tile_ref[t], 0.0))

    @pl.loop(0, tiles)
    def _(t):
        precondition_tile(t, b_ref[:, tile_lanes(t)], u_buf)

    mine = pl.ds(pl.multiple_of(core * hh, hh), hh)
    other = pl.ds(pl.multiple_of((1 - core) * hh, hh), hh)
    goes_up = jnp.logical_and(place >= my_col, place < depth - 1)
    goes_down = jnp.logical_and(place <= my_col, place > 0)
    per_chunk = steps // chunks

    def multiply_and_spread(turn, make, use):
        def swap(source, target, sem, column, q):
            return pltpu.make_async_remote_copy(
                src_ref=source, dst_ref=target, send_sem=sem.at[turn, 0, q], recv_sem=sem.at[turn, 1, q],
                device_id=(my_row, column), device_id_type=MESH,
            )

        def cut(q):
            return pl.ds(q * piece, piece)

        def first(q):
            return swap(part.at[turn, other, cut(q)], near.at[turn, :, cut(q)], near_sem, partner, q)

        def second(q):
            return swap(half.at[turn, :, cut(q)], far.at[turn, :, cut(q)], far_sem, across, q)

        def third(q):
            return swap(full.at[turn, mine, cut(q)], full.at[turn, mine, cut(q)], full_sem, partner, q)

        def lanes_of(owner, q):
            return pl.ds(pl.multiple_of(owner * block_rows + q * piece, width), piece)

        def along(q, way, target_row):
            return pltpu.make_async_remote_copy(
                src_ref=image.at[turn, :, lanes_of(lane, q)], dst_ref=image.at[turn, :, lanes_of(lane, q)],
                send_sem=line_send.at[turn, way, q], recv_sem=line_recv.at[turn, q],
                device_id=(target_row, my_col), device_id_type=MESH,
            )

        def sideways(q, shift, owner, side):
            return pltpu.make_async_remote_copy(
                src_ref=image.at[turn, :, lanes_of(owner, q)], dst_ref=image.at[turn, :, lanes_of(owner, q)],
                send_sem=side_send.at[turn, shift - 1, q], recv_sem=side_recv.at[turn, shift - 1, q],
                device_id=(side, my_col), device_id_type=MESH,
            )

        def outgoing(q, shift):
            return sideways(q, shift, lane, place * group + lax.rem(lane + shift, group))

        def pass_on(q):
            @pl.when(goes_up)
            def _():
                along(q, 0, my_row + group).start()

            @pl.when(goes_down)
            def _():
                along(q, 1, my_row - group).start()

            for shift in range(1, group):
                outgoing(q, shift).start()

        def stage0(q):
            @pl.loop(q * per_chunk, (q + 1) * per_chunk)
            def _(i):
                part[turn, :, tile_lanes(i)] = make(i)

            if turn == 0 and q == 0:
                pl.semaphore_wait(
                    barrier,
                    3 + (group - 1) + jnp.where(place > 0, 1, 0) + jnp.where(place < depth - 1, 1, 0),
                )
            first(q).start()

        def stage1(q):
            first(q).wait()
            half[turn, :, cut(q)] = part[turn, mine, cut(q)] + near[turn, :, cut(q)]
            second(q).start()

        def stage2(q):
            second(q).wait()
            full[turn, mine, cut(q)] = half[turn, :, cut(q)] + far[turn, :, cut(q)]
            third(q).start()

        def stage3(q):
            third(q).wait()

            @pl.when(place == my_col)
            def _():
                image[turn, :, lanes_of(lane, q)] = full[turn, :, cut(q)]
                pass_on(q)

        for tick in range(chunks + LAGS[-1]):
            for lag, stage in zip(LAGS, (stage0, stage1, stage2, stage3)):
                if 0 <= tick - lag < chunks:
                    stage(tick - lag)

        @pl.when(place != my_col)
        def _():
            for q in range(chunks):
                along(q, 0, my_row).wait_recv()
                pass_on(q)

        if turn == 1:
            for shift in range(1, 4):
                dots_copy(0, shift).wait()
        for q in range(chunks):
            use(lane * steps + q * per_chunk, per_chunk)
        for q in range(chunks):
            for shift in range(1, group):
                origin = lax.rem(lane + group - shift, group)
                sideways(q, shift, origin, place * group + origin).wait_recv()
                use(origin * steps + q * per_chunk, per_chunk)

        def finish():
            for q in range(chunks):
                @pl.when(goes_up)
                def _():
                    along(q, 0, my_row + group).wait_send()

                @pl.when(goes_down)
                def _():
                    along(q, 1, my_row - group).wait_send()

                for shift in range(1, group):
                    outgoing(q, shift).wait_send()

        return finish

    def dots_copy(turn, shift):
        return pltpu.make_async_remote_copy(
            src_ref=dot_own.at[turn], dst_ref=dot_in.at[turn, shift - 1],
            send_sem=dot_send.at[turn, shift - 1], recv_sem=dot_recv.at[turn, shift - 1],
            device_id=(my_row, lax.rem(my_col + shift, 4)), device_id_type=MESH,
        )

    def pack(gamma, delta):
        place_of = lax.broadcasted_iota(jnp.int32, (nrhs, width), 1)
        gamma = jnp.sum(gamma, axis=1, keepdims=True)
        delta = jnp.sum(delta, axis=1, keepdims=True)
        return jnp.where(place_of == 0, gamma, jnp.where(place_of == 1, delta, 0.0))

    def unpack(turn):
        total = [dot_own[turn]] + [dot_in[turn, (3 - my_col_shift)] for my_col_shift in (1, 2, 3)]
        total = (total[0] + total[2]) + (total[1] + total[3])
        return total[:, 0:1], total[:, 1:2]

    sums[...] = jnp.zeros_like(sums)

    def first_product(i):
        fetch(i).wait()
        parts = split(a_buf[i])
        a_split[i] = parts
        return fold(times_transposed(v_split[...], parts), nrhs, width)

    def second_product(i):
        return fold(times_transposed(v_split[...], a_split[i]), nrhs, width)

    def first_use(begin, count):
        @pl.loop(begin, begin + count)
        def _(t):
            lanes = tile_lanes(t)
            u, w = u_buf[:, lanes], image[0, :, lanes]
            sums[0] += b_ref[:, lanes] * u
            sums[1] += w * u
            precondition_tile(t, w, m_buf)

    finish_first = multiply_and_spread(0, first_product, first_use)
    dot_own[0] = pack(sums[0], sums[1])
    for shift in (2, 1, 3):
        dots_copy(0, shift).start()
    sums[...] = jnp.zeros_like(sums)

    def second_use(begin, count):
        gamma0, delta0 = unpack(0)
        alpha0 = gamma0 / delta0

        @pl.loop(begin, begin + count)
        def _(t):
            lanes = tile_lanes(t)
            w, u = image[0, :, lanes], u_buf[:, lanes]
            res = b_ref[:, lanes] - alpha0 * w
            pre = u - alpha0 * m_buf[:, lanes]
            img = w - alpha0 * image[1, :, lanes]
            res_ref[:, lanes] = res
            sol_ref[:, lanes] = alpha0 * u
            m_buf[:, lanes] = pre
            i_buf[:, lanes] = img
            sums[0] += res * pre
            sums[1] += img * pre

    finish_second = multiply_and_spread(1, second_product, second_use)
    dot_own[1] = pack(sums[0], sums[1])
    for shift in (2, 1, 3):
        dots_copy(1, shift).start()
    finish_first()
    finish_second()
    for shift in range(1, 4):
        dots_copy(1, shift).wait()
    gamma0, delta0 = unpack(0)
    alpha0 = gamma0 / delta0
    gamma1, delta1 = unpack(1)
    beta = gamma1 / gamma0
    alpha1 = gamma1 / (delta1 - beta * gamma1 / alpha0)

    @pl.loop(0, tiles)
    def _(t):
        lanes = tile_lanes(t)
        sol_ref[:, lanes] += alpha1 * (m_buf[:, lanes] + beta * u_buf[:, lanes])
        res_ref[:, lanes] -= alpha1 * (i_buf[:, lanes] + beta * image[0, :, lanes])


def fused_body(row_count, group, normal_matrix, right_side, tile_inverse, order_ids):
    block_rows, block_cols = normal_matrix.shape
    nrhs = right_side.shape[1]
    tiles, width = tile_inverse.shape[:2]
    steps = block_rows // width
    chunks = CHUNKS if steps % CHUNKS == 0 else 1
    f32, bf16 = jnp.float32, jnp.bfloat16
    out = jax.ShapeDtypeStruct((nrhs, block_cols), f32)
    dma = pltpu.SemaphoreType.DMA
    vmem = pl.BlockSpec(memory_space=pltpu.VMEM)
    sol, res = pl.pallas_call(
        functools.partial(kernel, row_count, group, chunks, width),
        out_shape=(out, out),
        in_specs=[pl.BlockSpec(memory_space=pl.ANY), vmem, vmem, vmem],
        out_specs=(vmem, vmem),
        scratch_shapes=[
            pltpu.VMEM((steps, width, block_cols), f32),
            pltpu.VMEM((steps, 2 * width, block_cols), bf16),
            pltpu.VMEM((tiles, 2 * width, width), bf16),
            pltpu.VMEM((2 * nrhs, block_cols), bf16),
            pltpu.VMEM((nrhs, block_cols), f32),
            pltpu.VMEM((nrhs, block_cols), f32),
            pltpu.VMEM((2, nrhs, block_rows), f32),
            pltpu.VMEM((2, nrhs // 2, block_rows), f32),
            pltpu.VMEM((2, nrhs // 2, block_rows), f32),
            pltpu.VMEM((2, nrhs // 2, block_rows), f32),
            pltpu.VMEM((2, nrhs, block_rows), f32),
            pltpu.VMEM((2, nrhs, block_cols), f32),
            pltpu.VMEM((2, nrhs, width), f32),
            pltpu.VMEM((2, 3, nrhs, width), f32),
            pltpu.VMEM((2, nrhs, width), f32),
            pltpu.VMEM((nrhs, block_cols), f32),
            pltpu.VMEM((width, width), f32),
            dma((steps,)),
            dma((2, 2, chunks)),
            dma((2, 2, chunks)),
            dma((2, 2, chunks)),
            dma((2, chunks)),
            dma((2, 2, chunks)),
            dma((2, group - 1, chunks)),
            dma((2, group - 1, chunks)),
            dma((2, 3)),
            dma((2, 3)),
        ],
        compiler_params=pltpu.CompilerParams(
            collective_id=0, has_side_effects=True, vmem_limit_bytes=60 * 1024 * 1024
        ),
    )(normal_matrix, tile_inverse, right_side.T, order_ids.reshape(tiles, width))
    return sol.T, res.T


def body(row_count, col_count, normal_matrix, right_side, tile_inverse, order_ids):
    block_rows, block_cols = normal_matrix.shape
    width = tile_inverse.shape[1]
    group = block_cols // block_rows
    fits = (
        col_count == 4
        and group > 1
        and row_count == group * col_count
        and block_rows % width == 0
        and width % 128 == 0
        and tile_inverse.shape[0] <= width
        and right_side.shape[1] % 32 == 0
    )
    if fits:
        return fused_body(row_count, group, normal_matrix, right_side, tile_inverse, order_ids)
    return plain_body(normal_matrix, right_side, tile_inverse, order_ids)


def solution(mesh):
    return jax.shard_map(
        functools.partial(body, mesh.shape["row"], mesh.shape["col"]),
        mesh=mesh,
        in_specs=(P("row", "col"), P("col", None), P("col", None, None), P("col")),
        out_specs=(P("col", None), P("col", None)),
        check_vma=False,
    )
```

profile of v0, /device:TPU:0, one launch (start us, length us, event | category | flops | bytes accessed | tf_op | source)
XLA Modules:
  0.0 63.6 jit_solution(13776741106202258781)
XLA Ops:
  0.6 59.1 %shard_map.59 = (f32[64,2304]{1,0:T(8,128)}, f32[64,2304]{1,0:T(8,128)}) custom-call(f32[1152,2304]{1,0:T(8,128)} %a_ref.1, f32[18,128,128]{2,1,0:T(8,128)} %tile_ref.1, f32[64,2304]{1,0:T(8,128)} %bitcast.4, s32[18,128]{1,0:T(8,128)} %bitcast.7), custom_call_target="tpu_custom_call" | custom-call | tf_op jit(solution)/shard_map/pallas_call | solution.py:387
  59.8 1.9 %copy.8 = f32[2304,64]{0,1:T(8,128)} copy(f32[2304,64]{0,1:T(8,128)} %bitcast.6) | data formatting | bytes 1179648
  61.7 1.9 %copy.9 = f32[2304,64]{0,1:T(8,128)} copy(f32[2304,64]{0,1:T(8,128)} %bitcast.5) | data formatting | bytes 1179648
where the time goes:
time: 63.8 us; the launch traced here: 63.6 us
  Pallas kernels  59.1 us (93%)
  local copies, waits for them, and re-layouts  3.83 us (6%)
  between operations  0.64 us (1%)
    pallas_call x1, Pallas kernels, fused_body(): pl.pallas_call(functools.partial(kernel, row_count, group, chunks, width)...  59.1 us
    unnamed x2, local copies, waits for them, and re-layouts  3.83 us

commit v1 on v0

v1 whole, which is shorter than its diff:
```python
import functools

import jax
import jax.numpy as jnp
from jax import lax
from jax.experimental import pallas as pl
from jax.experimental.pallas import tpu as pltpu
from jax.sharding import PartitionSpec as P

ITERS = 2
MESH = pl.DeviceIdType.MESH
NEAR_LAG = 3
OWN_LAG = 5
SIDE_LAG = 8


def masked_tiles(tile_inverse, order_ids):
    count = tile_inverse.shape[0]
    width = tile_inverse.shape[1]
    order_tile = order_ids.reshape(count, width)
    same_order = order_tile[:, :, None] == order_tile[:, None, :]
    return jnp.where(same_order, tile_inverse, jnp.float32(0.0))


def apply_precond(tile_inverse, order_ids, vector):
    count = tile_inverse.shape[0]
    width = tile_inverse.shape[1]
    masked = masked_tiles(tile_inverse, order_ids)
    pieces = vector.reshape(count, width, vector.shape[1])
    result = jnp.einsum("tij,tjk->tik", masked, pieces, precision=lax.Precision.HIGHEST)
    return result.reshape(vector.shape)


def plain_body(normal_matrix, right_side, tile_inverse, order_ids):
    block_rows = normal_matrix.shape[0]

    def apply_matrix(vector):
        first_row = lax.axis_index("row") * block_rows
        gathered = lax.all_gather(vector, "col", axis=0, tiled=True)
        row_piece = lax.dynamic_slice_in_dim(gathered, first_row, block_rows, 0)
        partial_value = lax.dot_general(
            normal_matrix,
            row_piece,
            (((0,), (0,)), ((), ())),
            precision=lax.Precision.HIGHEST,
            preferred_element_type=jnp.float32,
        )
        return lax.psum(partial_value, "row")

    solution = jnp.zeros_like(right_side)
    residual = right_side
    precond_res = apply_precond(tile_inverse, order_ids, residual)
    image_res = apply_matrix(precond_res)
    image_dir = jnp.zeros_like(right_side)
    precond_dir = jnp.zeros_like(right_side)
    residual_dir = jnp.zeros_like(right_side)
    direction = jnp.zeros_like(right_side)
    gamma_prev = jnp.ones((right_side.shape[1],), jnp.float32)
    alpha_prev = jnp.ones((right_side.shape[1],), jnp.float32)
    for iteration in range(ITERS):
        gamma_now, delta_now = lax.psum(
            (jnp.sum(residual * precond_res, axis=0), jnp.sum(image_res * precond_res, axis=0)),
            "col",
        )
        precond_img = apply_precond(tile_inverse, order_ids, image_res)
        image_img = apply_matrix(precond_img)
        if iteration == 0:
            beta_ratio = jnp.zeros_like(gamma_now)
            step_size = gamma_now / delta_now
        else:
            beta_ratio = gamma_now / gamma_prev
            step_size = gamma_now / (delta_now - beta_ratio * gamma_now / alpha_prev)
        image_dir = image_img + beta_ratio * image_dir
        precond_dir = precond_img + beta_ratio * precond_dir
        residual_dir = image_res + beta_ratio * residual_dir
        direction = precond_res + beta_ratio * direction
        solution = solution + step_size * direction
        residual = residual - step_size * residual_dir
        precond_res = precond_res - step_size * precond_dir
        image_res = image_res - step_size * image_dir
        gamma_prev = gamma_now
        alpha_prev = step_size
    return (solution, residual)


def halves(value):
    high = value.astype(jnp.bfloat16)
    low = (value - high.astype(jnp.float32)).astype(jnp.bfloat16)
    return high, low


def split(value):
    return jnp.concatenate(halves(value), axis=0)


def times(left, right):
    return lax.dot_general(
        left, right, (((1,), (0,)), ((), ())), preferred_element_type=jnp.float32
    )


def times_transposed(left, right):
    return lax.dot_general(
        left, right, (((1,), (1,)), ((), ())), preferred_element_type=jnp.float32
    )


def fold(product, rows, columns):
    both = product[:rows] + product[rows:]
    return both[:, :columns] + both[:, columns:]


def kernel(
    depth, width,
    a_ref, tile_ref, b_ref, ids_ref,
    u_out, m_out, w_out, n_out, s_out,
    a_buf, a_split, tile_buf, tile_split, v_split, m_split, b_buf, u_buf, m_buf,
    part, near, half, far, done, image, acc,
    sums, dot_own, dot_in, delta_own, delta_in, ids_buf,
    a_sem, in_sem, out_sem, near_sem, far_sem, line_sem, side_sem,
    near_send, far_send, fan_send, relay_send, dot_send, dot_recv, delta_send, delta_recv,
):
    my_row, my_col = lax.axis_index("row"), lax.axis_index("col")
    place, lane = my_row // 2, lax.rem(my_row, 2)
    core = lax.rem(my_col, 2)
    partner = my_col + 1 - 2 * core
    across = lax.rem(my_col + 2, 4)
    side = my_row + 1 - 2 * lane
    owner = place == my_col
    owner_chip = place // 2 == my_col // 2
    helper = jnp.logical_and(owner_chip, jnp.logical_not(owner))
    others = jnp.logical_not(owner)
    above, below = place < depth - 1, place > 0
    nrhs, block_cols = b_buf.shape
    block_rows = acc.shape[1]
    hh = nrhs // 2
    tiles = block_cols // width
    steps = block_rows // width
    mine = pl.ds(pl.multiple_of(core * hh, hh), hh)
    other = pl.ds(pl.multiple_of((1 - core) * hh, hh), hh)

    def fetch(i):
        return pltpu.make_async_copy(a_ref.at[pl.ds(i * width, width)], a_buf.at[i], a_sem.at[i])

    fetch_b = pltpu.make_async_copy(b_ref, b_buf, in_sem.at[0])
    fetch_tiles = pltpu.make_async_copy(tile_ref, tile_buf, in_sem.at[1])
    fetch_tiles.start()
    fetch_b.start()
    for i in range(steps):
        fetch(i).start()

    barrier = pltpu.get_barrier_semaphore()

    def greet(row, col):
        pl.semaphore_signal(barrier, inc=1, device_id=(row, col), device_id_type=MESH)

    for shift in range(1, 4):
        greet(my_row, lax.rem(my_col + shift, 4))
    greet(side, my_col)
    greet(2 * my_col + 1 - lane, my_col)

    @pl.when(others)
    def _():
        greet(2 * my_col + lane, my_col)

    @pl.when(place > my_col)
    def _():
        greet(my_row - 2, my_col)

    @pl.when(place < my_col)
    def _():
        greet(my_row + 2, my_col)

    @pl.when(jnp.logical_or(place == my_col + 1, place == my_col - 1))
    def _():
        greet(2 * my_col + lane, partner)

    @pl.when(owner)
    def _():
        greet(side, partner)

    goes_up = jnp.logical_and(place >= my_col, above)
    goes_down = jnp.logical_and(place <= my_col, below)

    def one(flag):
        return jnp.where(flag, 1, 0)

    def meet():
        awaited = 4 + one(goes_up) + one(goes_down)
        awaited += jnp.where(helper, 1 + one(above) + one(below), 0)
        awaited += jnp.where(owner, 2 * depth - 1, 0)
        pl.semaphore_wait(barrier, awaited)

    def lanes_at(t):
        return pl.ds(pl.multiple_of(t * width, width), width)

    def cut(q):
        return pl.ds(q * width, width)

    def lanes_of(block, q):
        return lanes_at(block * steps + q)

    def near_chunk(turn, q):
        return pltpu.make_async_remote_copy(
            src_ref=part.at[turn, other, cut(q)], dst_ref=near.at[turn, :, cut(q)],
            send_sem=near_send.at[turn], recv_sem=near_sem.at[turn, q],
            device_id=(my_row, partner), device_id_type=MESH,
        )

    def far_chunk(turn, q):
        return pltpu.make_async_remote_copy(
            src_ref=half.at[turn, :, cut(q)], dst_ref=far.at[turn, :, cut(q)],
            send_sem=far_send.at[turn], recv_sem=far_sem.at[turn, q],
            device_id=(my_row, across), device_id_type=MESH,
        )

    def fan_chunk(turn, q, way, row, sem):
        return pltpu.make_async_remote_copy(
            src_ref=done.at[turn, :, cut(q)], dst_ref=image.at[turn, mine, lanes_of(lane, q)],
            send_sem=fan_send.at[turn, way], recv_sem=sem.at[turn, q],
            device_id=(row, place), device_id_type=MESH,
        )

    def relay_chunk(turn, q, way, row, sem):
        return pltpu.make_async_remote_copy(
            src_ref=image.at[turn, :, lanes_of(lane, q)], dst_ref=image.at[turn, :, lanes_of(lane, q)],
            send_sem=relay_send.at[turn, way], recv_sem=sem.at[turn, q],
            device_id=(row, my_col), device_id_type=MESH,
        )

    def stage1(turn, q):
        near_chunk(turn, q).wait_recv()
        half[turn, :, cut(q)] = part[turn, mine, cut(q)] + near[turn, :, cut(q)]

        @pl.when(jnp.logical_not(owner_chip))
        def _():
            far_chunk(turn, q).start()

    def stage2(turn, q):
        @pl.when(owner_chip)
        def _():
            far_chunk(turn, q).wait_recv()
            total = half[turn, :, cut(q)] + far[turn, :, cut(q)]
            done[turn, :, cut(q)] = total

            @pl.when(above)
            def _():
                fan_chunk(turn, q, 0, my_row + 2, line_sem).start()

            @pl.when(below)
            def _():
                fan_chunk(turn, q, 1, my_row - 2, line_sem).start()

            fan_chunk(turn, q, 2, side, side_sem).start()

            @pl.when(helper)
            def _():
                fan_chunk(turn, q, 3, my_row, line_sem).start()

            @pl.when(owner)
            def _():
                image[turn, mine, lanes_of(lane, q)] = total

    def own(turn, q):
        @pl.when(owner)
        def _():
            pltpu.make_async_remote_copy(
                src_ref=done.at[turn, :, cut(q)], dst_ref=image.at[turn, other, lanes_of(lane, q)],
                send_sem=fan_send.at[turn, 3], recv_sem=line_sem.at[turn, q],
                device_id=(my_row, partner), device_id_type=MESH,
            ).wait_recv()

        @pl.when(others)
        def _():
            relay_chunk(turn, q, 0, my_row, line_sem).wait_recv()

            @pl.when(goes_up)
            def _():
                relay_chunk(turn, q, 0, my_row + 2, line_sem).start()

            @pl.when(goes_down)
            def _():
                relay_chunk(turn, q, 0, my_row - 2, line_sem).start()

            relay_chunk(turn, q, 1, side, side_sem).start()

    def beside(turn, q):
        pltpu.make_async_remote_copy(
            src_ref=image.at[turn, :, lanes_of(1 - lane, q)], dst_ref=image.at[turn, :, lanes_of(1 - lane, q)],
            send_sem=relay_send.at[turn, 1], recv_sem=side_sem.at[turn, q],
            device_id=(side, my_col), device_id_type=MESH,
        ).wait_recv()

    def finish(turn):
        near_all = pltpu.make_async_remote_copy(
            src_ref=part.at[turn, other], dst_ref=near.at[turn],
            send_sem=near_send.at[turn], recv_sem=near_sem.at[turn, 0],
            device_id=(my_row, partner), device_id_type=MESH,
        )
        near_all.wait_send()

        def fan_all(way):
            return pltpu.make_async_remote_copy(
                src_ref=done.at[turn], dst_ref=far.at[turn],
                send_sem=fan_send.at[turn, way], recv_sem=line_sem.at[turn, 0],
                device_id=(side, my_col), device_id_type=MESH,
            )

        def relay_all(way):
            return pltpu.make_async_remote_copy(
                src_ref=part.at[turn], dst_ref=part.at[turn],
                send_sem=relay_send.at[turn, way], recv_sem=line_sem.at[turn, 0],
                device_id=(side, my_col), device_id_type=MESH,
            )

        @pl.when(jnp.logical_not(owner_chip))
        def _():
            pltpu.make_async_remote_copy(
                src_ref=half.at[turn], dst_ref=far.at[turn],
                send_sem=far_send.at[turn], recv_sem=far_sem.at[turn, 0],
                device_id=(my_row, across), device_id_type=MESH,
            ).wait_send()

        @pl.when(owner_chip)
        def _():
            @pl.when(above)
            def _():
                fan_all(0).wait_send()

            @pl.when(below)
            def _():
                fan_all(1).wait_send()

            fan_all(2).wait_send()

            @pl.when(helper)
            def _():
                fan_all(3).wait_send()

        @pl.when(others)
        def _():
            @pl.when(jnp.logical_or(goes_up, goes_down))
            def _():
                relay_all(0).wait_send()

            relay_all(1).wait_send()

    def dot_row():
        return jnp.sum(sums[...].T, axis=0, keepdims=True)

    def exchange(turn, row):
        dot_own[turn] = jnp.broadcast_to(row, dot_own.shape[1:])
        for shift in (2, 1, 3):
            pltpu.make_async_remote_copy(
                src_ref=dot_own.at[turn], dst_ref=dot_in.at[turn, shift - 1],
                send_sem=dot_send.at[turn], recv_sem=dot_recv.at[turn],
                device_id=(my_row, lax.rem(my_col + shift, 4)), device_id_type=MESH,
            ).start()

    def exchanged(turn):
        pltpu.make_async_remote_copy(
            src_ref=dot_in.at[turn], dst_ref=dot_in.at[turn],
            send_sem=dot_send.at[turn], recv_sem=dot_recv.at[turn],
            device_id=(my_row, partner), device_id_type=MESH,
        ).wait()
        total = (dot_own[turn] + dot_in[turn, 1]) + (dot_in[turn, 0] + dot_in[turn, 2])
        across_lanes = jnp.broadcast_to(total[0:1], (2 * nrhs, width)).T
        return across_lanes[:nrhs], across_lanes[nrhs:]

    ids_buf[...] = jnp.zeros_like(ids_buf)
    ids_buf[0:tiles] = ids_ref[...].astype(jnp.float32)
    ids_across = ids_buf[...].T
    fetch_tiles.wait()
    for t in range(tiles):
        same = ids_across[:, t : t + 1] == ids_buf[t : t + 1]
        tile_split[t] = jnp.concatenate(halves(jnp.where(same, tile_buf[t], 0.0)), axis=1)
    fetch_b.wait()
    gamma = jnp.zeros((nrhs, width), jnp.float32)
    for t in range(tiles):
        value = b_buf[:, cut(t)]
        product = fold(times(split(value), tile_split[t]), nrhs, width)
        u_buf[:, cut(t)] = product
        v_split[:, cut(t)] = split(product)
        gamma += value * product
    sums[:nrhs] = gamma
    sums[nrhs:] = jnp.zeros_like(gamma)

    for q in range(steps):
        fetch(q).wait()
        a_split[q] = split(a_buf[q])
        part[0, :, cut(q)] = fold(times_transposed(v_split[...], a_split[q]), nrhs, width)
        if q == 0:
            meet()
        near_chunk(0, q).start()
        if q >= NEAR_LAG:
            stage1(0, q - NEAR_LAG)
    for q in range(steps - NEAR_LAG, steps):
        stage1(0, q)
    write_u = pltpu.make_async_copy(u_buf, u_out, out_sem.at[0])
    write_u.start()

    acc[...] = jnp.zeros_like(acc)

    def take(block, q, slot):
        lanes = lanes_of(block, q)
        value = image[0, :, lanes]
        product = fold(times(split(value), tile_split[block * steps + q]), nrhs, width)
        m_buf[:, lanes] = product
        m_split[slot] = split(product)
        sums[nrhs:] += value * u_buf[:, lanes]
        return slot, lanes

    def update(taken, i):
        product = None
        for slot, lanes in taken:
            term = times_transposed(m_split[slot], a_split[i, :, lanes])
            product = term if product is None else product + term
        return acc[:, cut(i)] + fold(product, nrhs, width)

    taken = []
    for tick in range(steps + SIDE_LAG):
        if tick < steps:
            stage2(0, tick)
        q, r = tick - OWN_LAG, tick - SIDE_LAG
        if 0 <= q < steps:
            own(0, q)
        if 0 <= r < steps:
            beside(0, r)
        if taken:
            for i in range(steps):
                acc[:, cut(i)] = update(taken, i)
        slot = 2 * (tick % 2)
        taken = []
        if 0 <= q < steps:
            taken.append(take(lane, q, slot))
        if 0 <= r < steps:
            taken.append(take(1 - lane, r, slot + 1))
    for i in range(steps):
        part[1, :, cut(i)] = update(taken, i)
        near_chunk(1, i).start()
    exchange(0, dot_row())
    write_m = pltpu.make_async_copy(m_buf, m_out, out_sem.at[1])
    write_m.start()
    write_w = pltpu.make_async_copy(image.at[0], w_out, out_sem.at[2])
    write_w.start()
    for q in range(steps):
        stage1(1, q)
    gamma0, delta0 = exchanged(0)
    alpha0 = gamma0 / delta0
    gamma = jnp.zeros((nrhs, width), jnp.float32)
    for t in range(tiles):
        lanes = cut(t)
        res = b_buf[:, lanes] - alpha0 * image[0, :, lanes]
        pre = u_buf[:, lanes] - alpha0 * m_buf[:, lanes]
        gamma += res * pre
    sums[:nrhs] = gamma
    sums[nrhs:] = jnp.zeros_like(gamma)

    def write_n(block, q):
        lanes = lanes_of(block, q)
        return pltpu.make_async_copy(image.at[1, :, lanes], n_out.at[:, lanes], out_sem.at[3])

    def deltas():
        row = dot_row()
        upper = lax.broadcasted_iota(jnp.int32, (1, width), 1) >= nrhs

        @pl.when(owner)
        def _():
            message = jnp.broadcast_to(jnp.where(upper, row, 0.0), delta_in.shape[1:])
            delta_in[lane] = message
            for i in range(2 * depth - 1):
                delta_own[i] = message
                pltpu.make_async_remote_copy(
                    src_ref=delta_own.at[i], dst_ref=delta_in.at[lane],
                    send_sem=delta_send.at[0], recv_sem=delta_recv.at[0],
                    device_id=(lax.rem(my_row + i + 1, 2 * depth), my_col), device_id_type=MESH,
                ).start()

        return row, upper

    for tick in range(steps + SIDE_LAG):
        if tick < steps:
            stage2(1, tick)
        q, r = tick - OWN_LAG, tick - SIDE_LAG
        if 0 <= q < steps:
            own(1, q)
            write_n(lane, q).start()

            @pl.when(owner)
            def _():
                lanes = lanes_of(lane, q)
                img = image[0, :, lanes] - alpha0 * image[1, :, lanes]
                sums[nrhs:] += img * (u_buf[:, lanes] - alpha0 * m_buf[:, lanes])

        if q == steps - 1:
            row, upper = deltas()
        if 0 <= r < steps:
            beside(1, r)
            write_n(1 - lane, r).start()

    def delta_copy(slots):
        return pltpu.make_async_remote_copy(
            src_ref=slots, dst_ref=slots, send_sem=delta_send.at[0], recv_sem=delta_recv.at[0],
            device_id=(side, my_col), device_id_type=MESH,
        )

    @pl.when(owner)
    def _():
        delta_copy(delta_in.at[1 - lane]).wait_recv()

    @pl.when(others)
    def _():
        delta_copy(delta_in).wait_recv()

    exchange(1, jnp.where(upper, (delta_in[0] + delta_in[1])[0:1], row))
    finish(0)
    finish(1)
    write_u.wait()
    write_m.wait()
    write_w.wait()
    pltpu.make_async_copy(image.at[1], n_out, out_sem.at[3]).wait()

    @pl.when(owner)
    def _():
        delta_copy(delta_own).wait_send()

    gamma1, delta1 = exchanged(1)
    beta = gamma1 / gamma0
    s_out[0] = alpha0
    s_out[1] = gamma1 / (delta1 - beta * gamma1 / alpha0)
    s_out[2] = beta


def fused_body(row_count, normal_matrix, right_side, tile_inverse, order_ids):
    block_rows, block_cols = normal_matrix.shape
    nrhs = right_side.shape[1]
    tiles, width = tile_inverse.shape[:2]
    steps = block_rows // width
    depth = row_count // 2
    f32, bf16 = jnp.float32, jnp.bfloat16
    whole = jax.ShapeDtypeStruct((nrhs, block_cols), f32)
    dma = pltpu.SemaphoreType.DMA
    vmem = pl.BlockSpec(memory_space=pltpu.VMEM)
    hbm = pl.BlockSpec(memory_space=pl.ANY)
    hh = nrhs // 2
    b = right_side.T
    u, m, w, n, scalars = pl.pallas_call(
        functools.partial(kernel, depth, width),
        out_shape=(whole, whole, whole, whole, jax.ShapeDtypeStruct((3, nrhs, width), f32)),
        in_specs=[hbm, hbm, hbm, vmem],
        out_specs=(hbm, hbm, hbm, hbm, vmem),
        scratch_shapes=[
            pltpu.VMEM((steps, width, block_cols), f32),
            pltpu.VMEM((steps, 2 * width, block_cols), bf16),
            pltpu.VMEM((tiles, width, width), f32),
            pltpu.VMEM((tiles, width, 2 * width), bf16),
            pltpu.VMEM((2 * nrhs, block_cols), bf16),
            pltpu.VMEM((4, 2 * nrhs, width), bf16),
            pltpu.VMEM((nrhs, block_cols), f32),
            pltpu.VMEM((nrhs, block_cols), f32),
            pltpu.VMEM((nrhs, block_cols), f32),
            pltpu.VMEM((2, nrhs, block_rows), f32),
            pltpu.VMEM((2, hh, block_rows), f32),
            pltpu.VMEM((2, hh, block_rows), f32),
            pltpu.VMEM((2, hh, block_rows), f32),
            pltpu.VMEM((2, hh, block_rows), f32),
            pltpu.VMEM((2, nrhs, block_cols), f32),
            pltpu.VMEM((nrhs, block_rows), f32),
            pltpu.VMEM((2 * nrhs, width), f32),
            pltpu.VMEM((2, 8, width), f32),
            pltpu.VMEM((2, 3, 8, width), f32),
            pltpu.VMEM((2 * depth - 1, 8, width), f32),
            pltpu.VMEM((2, 8, width), f32),
            pltpu.VMEM((width, width), f32),
            dma((steps,)),
            dma((2,)),
            dma((4,)),
            dma((2, steps)),
            dma((2, steps)),
            dma((2, steps)),
            dma((2, steps)),
            dma((2,)),
            dma((2,)),
            dma((2, 4)),
            dma((2, 2)),
            dma((2,)),
            dma((2,)),
            dma((1,)),
            dma((1,)),
        ],
        compiler_params=pltpu.CompilerParams(
            collective_id=0, has_side_effects=True, vmem_limit_bytes=60 * 1024 * 1024
        ),
    )(normal_matrix, tile_inverse, b, order_ids.reshape(tiles, width))
    alpha0, alpha1, beta = scalars[0, :, :1], scalars[1, :, :1], scalars[2, :, :1]
    pre = u - alpha0 * m
    sol = alpha0 * u + alpha1 * (pre + beta * u)
    res = (b - alpha0 * w) - alpha1 * ((w - alpha0 * n) + beta * w)
    return sol.T, res.T


def body(row_count, col_count, normal_matrix, right_side, tile_inverse, order_ids):
    block_rows, block_cols = normal_matrix.shape
    width = tile_inverse.shape[1]
    fits = (
        col_count == 4
        and row_count == 8
        and block_cols == 2 * block_rows
        and block_rows % width == 0
        and width == 128
        and tile_inverse.shape[0] <= width
        and right_side.shape[1] == 64
    )
    if fits:
        return fused_body(row_count, normal_matrix, right_side, tile_inverse, order_ids)
    return plain_body(normal_matrix, right_side, tile_inverse, order_ids)


def solution(mesh):
    return jax.shard_map(
        functools.partial(body, mesh.shape["row"], mesh.shape["col"]),
        mesh=mesh,
        in_specs=(P("row", "col"), P("col", None), P("col", None, None), P("col")),
        out_specs=(P("col", None), P("col", None)),
        check_vma=False,
    )
```

time: 63.8 us -> 63.1 us (0.989)
  other arithmetic: 0 us -> 2.97 us
  local copies, waits for them, and re-layouts: 3.83 us -> 0.94 us
  Pallas kernels: 59.1 us -> 58.3 us
    unnamed x2, local copies, waits for them, and re-layouts: 3.83 us -> 0.01 us
    transpose x0 -> x1, other arithmetic: none -> 2.97 us  [fused_body(): return (sol.T, res.T)]
    slice x0 -> x1, local copies, waits for them, and re-layouts: none -> 0.94 us  [fused_body(): scalars[0, :, :1]]
    pallas_call x1, Pallas kernels: 59.1 us -> 58.3 us  [fused_body(): pl.pallas_call(functools.partial(kernel, depth, width), out_shape=(whole,...]
where the time goes in v1:
time: 63.1 us; the launch traced here: 62.8 us
  Pallas kernels  58.3 us (92%)
  other arithmetic  2.97 us (5%)
  local copies, waits for them, and re-layouts  0.94 us (1%)
  between operations  0.65 us (1%)
    pallas_call x1, Pallas kernels, fused_body(): pl.pallas_call(functools.partial(kernel, depth, width), out_shape=(whole,...  58.3 us
    transpose x1, other arithmetic, fused_body(): return (sol.T, res.T)  2.97 us

profile of v1, /device:TPU:0, one launch (start us, length us, event | category | flops | bytes accessed | tf_op | source)
XLA Modules:
  0.0 62.8 jit_solution(6145479783235342892)
XLA Ops:
  0.6 0.0 copy-start
  0.6 58.3 %shard_map.59 = (f32[64,2304]{1,0:T(8,128)}, f32[64,2304]{1,0:T(8,128)}, f32[64,2304]{1,0:T(8,128)}, f32[64,2304]{1,0:T(8,128)}, f32[3,64,128]{2,1,0:T(8,128)}) custom-call(f32[1152,2304]{1,0:T(8,128)} %a_ref.1, f32[18,128,128]{2,1,0:T(8,128)} %tile_ref.1, f32[64,2304]{1,0:T(8,128)} %bitcast.7, s32[18,128]{1,0:T(8,128)} %bitcast.8), custom_call_target="tpu_custom_call" | custom-call | tf_op jit(solution)/shard_map/pallas_call | solution.py:547
  58.9 0.9 %slice_reduce_fusion.2 = (f32[64]{0:T(128)S(1)}, f32[64]{0:T(128)S(1)}, f32[64]{0:T(128)S(1)}) fusion(f32[3,64,128]{2,1,0:T(8,128)} %get-tuple-element.7), kind=kLoop, calls=%fused_computation.4 | loop fusion | bytes 1536 | tf_op jit(solution)/shard_map/slice | solution.py:595
  59.8 0.0 copy-done
  59.9 3.0 %subtract_bitcast_fusion = (f32[2304,64]{0,1:T(8,128)}, f32[2304,64]{0,1:T(8,128)}) fusion(f32[64,2304]{1,0:T(8,128)} %get-tuple-element.10, f32[64,2304]{1,0:T(8,128)} %get-tuple-element.11, f32[64]{0:T(128)S(1)} %get-tuple-element.13, f32[64]{0:T(128)S(1)} %get-tuple-element.14, f32[64]{0:T(128)S(1)} %get-tuple-element.12, f32[2304,64]{0,1:T(8,128)S(1)} %copy-done, ...), kind=kLoop, calls=%fused_computation | loop fusion | flops 2211840 | bytes 4129536 | tf_op jit(solution)/shard_map/transpose | solution.py:599
Async XLA Ops:
  0.6 59.2 %copy-start = (f32[2304,64]{0,1:T(8,128)S(1)}, f32[2304,64]{0,1:T(8,128)}, u32[]{:S(2)}) copy-start(f32[2304,64]{0,1:T(8,128)} %param.5) | copy-start | bytes 1769476

commit v2 on v1

--- a/solution.py
+++ b/solution.py
@@ -10,8 +10,6 @@
 ITERS = 2
 MESH = pl.DeviceIdType.MESH
 NEAR_LAG = 3
-OWN_LAG = 5
-SIDE_LAG = 8
 
 
 def masked_tiles(tile_inverse, order_ids):
@@ -113,11 +111,11 @@
 def kernel(
     depth, width,
     a_ref, tile_ref, b_ref, ids_ref,
-    u_out, m_out, w_out, n_out, s_out,
-    a_buf, a_split, tile_buf, tile_split, v_split, m_split, b_buf, u_buf, m_buf,
+    sol_ref, res_ref,
+    a_buf, a_split, tile_buf, tile_split, v_split, v_minus, m_split, b_buf, u_buf, m_buf,
     part, near, half, far, done, image, acc,
-    sums, dot_own, dot_in, delta_own, delta_in, ids_buf,
-    a_sem, in_sem, out_sem, near_sem, far_sem, line_sem, side_sem,
+    sums, dot_own, dot_in, delta_own, delta_fill, delta_in, ids_buf,
+    a_sem, in_sem, near_sem, far_sem, line_sem, side_sem,
     near_send, far_send, fan_send, relay_send, dot_send, dot_recv, delta_send, delta_recv,
 ):
     my_row, my_col = lax.axis_index("row"), lax.axis_index("col")
@@ -142,12 +140,16 @@
     def fetch(i):
         return pltpu.make_async_copy(a_ref.at[pl.ds(i * width, width)], a_buf.at[i], a_sem.at[i])
 
-    fetch_b = pltpu.make_async_copy(b_ref, b_buf, in_sem.at[0])
-    fetch_tiles = pltpu.make_async_copy(tile_ref, tile_buf, in_sem.at[1])
-    fetch_tiles.start()
+    first_tiles = tiles // 2
+    pieces = (pl.ds(0, first_tiles), pl.ds(first_tiles, tiles - first_tiles))
+
+    def fetch_tiles(k):
+        return pltpu.make_async_copy(tile_ref.at[pieces[k]], tile_buf.at[pieces[k]], in_sem.at[k])
+
+    fetch_b = pltpu.make_async_copy(b_ref, b_buf, in_sem.at[2])
+    fetch_tiles(0).start()
+    fetch_tiles(1).start()
     fetch_b.start()
-    for i in range(steps):
-        fetch(i).start()
 
     barrier = pltpu.get_barrier_semaphore()
 
@@ -370,34 +372,51 @@
     ids_buf[...] = jnp.zeros_like(ids_buf)
     ids_buf[0:tiles] = ids_ref[...].astype(jnp.float32)
     ids_across = ids_buf[...].T
-    fetch_tiles.wait()
+    fetch(0).start()
+    fetch_tiles(0).wait()
+    fetch(1).start()
+    fetch(2).start()
     for t in range(tiles):
+        if t == first_tiles:
+            fetch_tiles(1).wait()
+            fetch_b.wait()
+            for i in range(3, steps):
+                fetch(i).start()
         same = ids_across[:, t : t + 1] == ids_buf[t : t + 1]
         tile_split[t] = jnp.concatenate(halves(jnp.where(same, tile_buf[t], 0.0)), axis=1)
-    fetch_b.wait()
     gamma = jnp.zeros((nrhs, width), jnp.float32)
     for t in range(tiles):
         value = b_buf[:, cut(t)]
         product = fold(times(split(value), tile_split[t]), nrhs, width)
         u_buf[:, cut(t)] = product
-        v_split[:, cut(t)] = split(product)
+        parts = split(product)
+        v_split[:, cut(t)] = parts
+        v_minus[:, cut(t)] = -parts
         gamma += value * product
     sums[:nrhs] = gamma
     sums[nrhs:] = jnp.zeros_like(gamma)
 
-    for q in range(steps):
-        fetch(q).wait()
-        a_split[q] = split(a_buf[q])
-        part[0, :, cut(q)] = fold(times_transposed(v_split[...], a_split[q]), nrhs, width)
-        if q == 0:
+    met = False
+    halved = 0
+    for begin in [0] + list(range(1, steps, 2)):
+        group = range(begin, min(begin + 2, steps)) if begin else range(1)
+        for q in group:
+            fetch(q).wait()
+        for q in group:
+            a_split[q] = split(a_buf[q])
+            high = times_transposed(v_split[...], a_split[q, :width])
+            minus_low = times_transposed(v_minus[...], a_split[q, width:])
+            part[0, :, cut(q)] = (high[:nrhs] - minus_low[:nrhs]) + (high[nrhs:] - minus_low[nrhs:])
+        if not met:
             meet()
-        near_chunk(0, q).start()
-        if q >= NEAR_LAG:
-            stage1(0, q - NEAR_LAG)
-    for q in range(steps - NEAR_LAG, steps):
+            met = True
+        for q in group:
+            near_chunk(0, q).start()
+        while halved <= group[-1] - NEAR_LAG:
+            stage1(0, halved)
+            halved += 1
+    for q in range(halved, steps):
         stage1(0, q)
-    write_u = pltpu.make_async_copy(u_buf, u_out, out_sem.at[0])
-    write_u.start()
 
     acc[...] = jnp.zeros_like(acc)
 
@@ -417,32 +436,25 @@
             product = term if product is None else product + term
         return acc[:, cut(i)] + fold(product, nrhs, width)
 
+    for q in range(steps):
+        stage2(0, q)
+    arrivals = [(lane, q) for q in range(steps)] + [(1 - lane, q) for q in range(steps)]
     taken = []
-    for tick in range(steps + SIDE_LAG):
-        if tick < steps:
-            stage2(0, tick)
-        q, r = tick - OWN_LAG, tick - SIDE_LAG
-        if 0 <= q < steps:
-            own(0, q)
-        if 0 <= r < steps:
-            beside(0, r)
+    for begin in range(0, 2 * steps, 2):
+        for k in (begin, begin + 1):
+            if k < steps:
+                own(0, k)
+            else:
+                beside(0, k - steps)
         if taken:
             for i in range(steps):
                 acc[:, cut(i)] = update(taken, i)
-        slot = 2 * (tick % 2)
-        taken = []
-        if 0 <= q < steps:
-            taken.append(take(lane, q, slot))
-        if 0 <= r < steps:
-            taken.append(take(1 - lane, r, slot + 1))
+        taken = [take(*arrivals[k], k % 4) for k in (begin, begin + 1)]
     for i in range(steps):
         part[1, :, cut(i)] = update(taken, i)
+    for i in range(steps):
         near_chunk(1, i).start()
     exchange(0, dot_row())
-    write_m = pltpu.make_async_copy(m_buf, m_out, out_sem.at[1])
-    write_m.start()
-    write_w = pltpu.make_async_copy(image.at[0], w_out, out_sem.at[2])
-    write_w.start()
     for q in range(steps):
         stage1(1, q)
     gamma0, delta0 = exchanged(0)
@@ -455,48 +467,42 @@
         gamma += res * pre
     sums[:nrhs] = gamma
     sums[nrhs:] = jnp.zeros_like(gamma)
-
-    def write_n(block, q):
-        lanes = lanes_of(block, q)
-        return pltpu.make_async_copy(image.at[1, :, lanes], n_out.at[:, lanes], out_sem.at[3])
+    exchange(1, dot_row())
+
+    rows = 2 * depth
+
+    def slot_of(origin, target):
+        return lax.rem(origin - target + rows, rows)
 
     def deltas():
-        row = dot_row()
-        upper = lax.broadcasted_iota(jnp.int32, (1, width), 1) >= nrhs
-
         @pl.when(owner)
         def _():
-            message = jnp.broadcast_to(jnp.where(upper, row, 0.0), delta_in.shape[1:])
-            delta_in[lane] = message
-            for i in range(2 * depth - 1):
-                delta_own[i] = message
-                pltpu.make_async_remote_copy(
-                    src_ref=delta_own.at[i], dst_ref=delta_in.at[lane],
-                    send_sem=delta_send.at[0], recv_sem=delta_recv.at[0],
-                    device_id=(lax.rem(my_row + i + 1, 2 * depth), my_col), device_id_type=MESH,
-                ).start()
-
-        return row, upper
-
-    for tick in range(steps + SIDE_LAG):
-        if tick < steps:
-            stage2(1, tick)
-        q, r = tick - OWN_LAG, tick - SIDE_LAG
-        if 0 <= q < steps:
-            own(1, q)
-            write_n(lane, q).start()
-
-            @pl.when(owner)
-            def _():
-                lanes = lanes_of(lane, q)
-                img = image[0, :, lanes] - alpha0 * image[1, :, lanes]
-                sums[nrhs:] += img * (u_buf[:, lanes] - alpha0 * m_buf[:, lanes])
-
-        if q == steps - 1:
-            row, upper = deltas()
-        if 0 <= r < steps:
-            beside(1, r)
-            write_n(1 - lane, r).start()
+            delta_own[...] = jnp.broadcast_to(dot_row(), delta_own.shape)
+            delta_in[0] = delta_own[...]
+            for i in range(rows):
+                target = lax.rem(my_row + i, rows)
+                for shift in range(4):
+                    if i or shift:
+                        pltpu.make_async_remote_copy(
+                            src_ref=delta_own, dst_ref=delta_in.at[slot_of(my_row, target)],
+                            send_sem=delta_send.at[0], recv_sem=delta_recv.at[0],
+                            device_id=(target, lax.rem(my_col + shift, 4)), device_id_type=MESH,
+                        ).start()
+
+    for q in range(steps):
+        stage2(1, q)
+    for q in range(steps):
+        own(1, q)
+
+        @pl.when(owner)
+        def _():
+            lanes = lanes_of(lane, q)
+            img = image[0, :, lanes] - alpha0 * image[1, :, lanes]
+            sums[nrhs:] += img * (u_buf[:, lanes] - alpha0 * m_buf[:, lanes])
+
+    deltas()
+    for q in range(steps):
+        beside(1, q)
 
     def delta_copy(slots):
         return pltpu.make_async_remote_copy(
@@ -504,31 +510,32 @@
             device_id=(side, my_col), device_id_type=MESH,
         )
 
+    finish(0)
+    finish(1)
+
     @pl.when(owner)
     def _():
-        delta_copy(delta_in.at[1 - lane]).wait_recv()
+        delta_copy(delta_fill).wait_send()
+        delta_copy(delta_in.at[pl.ds(1, rows - 1)]).wait_recv()
 
     @pl.when(others)
     def _():
         delta_copy(delta_in).wait_recv()
 
-    exchange(1, jnp.where(upper, (delta_in[0] + delta_in[1])[0:1], row))
-    finish(0)
-    finish(1)
-    write_u.wait()
-    write_m.wait()
-    write_w.wait()
-    pltpu.make_async_copy(image.at[1], n_out, out_sem.at[3]).wait()
-
-    @pl.when(owner)
-    def _():
-        delta_copy(delta_own).wait_send()
-
-    gamma1, delta1 = exchanged(1)
+    gamma1 = exchanged(1)[0]
+    total = delta_in[slot_of(0, my_row)]
+    for origin in range(1, rows):
+        total = total + delta_in[slot_of(origin, my_row)]
+    delta1 = jnp.broadcast_to(total[0:1], (2 * nrhs, width)).T[nrhs:]
     beta = gamma1 / gamma0
-    s_out[0] = alpha0
-    s_out[1] = gamma1 / (delta1 - beta * gamma1 / alpha0)
-    s_out[2] = beta
+    alpha1 = gamma1 / (delta1 - beta * gamma1 / alpha0)
+    for t in range(tiles):
+        lanes = cut(t)
+        u, w = u_buf[:, lanes], image[0, :, lanes]
+        pre = u - alpha0 * m_buf[:, lanes]
+        img = w - alpha0 * image[1, :, lanes]
+        sol_ref[:, lanes] = alpha0 * u + alpha1 * (pre + beta * u)
+        res_ref[:, lanes] = (b_buf[:, lanes] - alpha0 * w) - alpha1 * (img + beta * w)
 
 
 def fused_body(row_count, normal_matrix, right_side, tile_inverse, order_ids):
@@ -541,19 +548,19 @@
     whole = jax.ShapeDtypeStruct((nrhs, block_cols), f32)
     dma = pltpu.SemaphoreType.DMA
     vmem = pl.BlockSpec(memory_space=pltpu.VMEM)
-    hbm = pl.BlockSpec(memory_space=pl.ANY)
+    hbm = pl.BlockSpec(memory_space=pltpu.HBM)
     hh = nrhs // 2
-    b = right_side.T
-    u, m, w, n, scalars = pl.pallas_call(
+    sol, res = pl.pallas_call(
         functools.partial(kernel, depth, width),
-        out_shape=(whole, whole, whole, whole, jax.ShapeDtypeStruct((3, nrhs, width), f32)),
+        out_shape=(whole, whole),
         in_specs=[hbm, hbm, hbm, vmem],
-        out_specs=(hbm, hbm, hbm, hbm, vmem),
+        out_specs=(vmem, vmem),
         scratch_shapes=[
             pltpu.VMEM((steps, width, block_cols), f32),
             pltpu.VMEM((steps, 2 * width, block_cols), bf16),
             pltpu.VMEM((tiles, width, width), f32),
             pltpu.VMEM((tiles, width, 2 * width), bf16),
+            pltpu.VMEM((2 * nrhs, block_cols), bf16),
             pltpu.VMEM((2 * nrhs, block_cols), bf16),
             pltpu.VMEM((4, 2 * nrhs, width), bf16),
             pltpu.VMEM((nrhs, block_cols), f32),
@@ -569,12 +576,12 @@
             pltpu.VMEM((2 * nrhs, width), f32),
             pltpu.VMEM((2, 8, width), f32),
             pltpu.VMEM((2, 3, 8, width), f32),
-            pltpu.VMEM((2 * depth - 1, 8, width), f32),
-            pltpu.VMEM((2, 8, width), f32),
+            pltpu.VMEM((8, width), f32),
+            pltpu.VMEM((8 * depth - 1, 8, width), f32),
+            pltpu.VMEM((2 * depth, 8, width), f32),
             pltpu.VMEM((width, width), f32),
             dma((steps,)),
-            dma((2,)),
-            dma((4,)),
+            dma((3,)),
             dma((2, steps)),
             dma((2, steps)),
             dma((2, steps)),
@@ -589,13 +596,9 @@
             dma((1,)),
         ],
         compiler_params=pltpu.CompilerParams(
-            collective_id=0, has_side_effects=True, vmem_limit_bytes=60 * 1024 * 1024
+            collective_id=0, has_side_effects=True, vmem_limit_bytes=53500 * 1024
         ),
-    )(normal_matrix, tile_inverse, b, order_ids.reshape(tiles, width))
-    alpha0, alpha1, beta = scalars[0, :, :1], scalars[1, :, :1], scalars[2, :, :1]
-    pre = u - alpha0 * m
-    sol = alpha0 * u + alpha1 * (pre + beta * u)
-    res = (b - alpha0 * w) - alpha1 * ((w - alpha0 * n) + beta * w)
+    )(normal_matrix, tile_inverse, right_side.T, order_ids.reshape(tiles, width))
     return sol.T, res.T
 
 

time: 63.1 us -> 46.2 us (0.73)
  the two profiles are of different devices: /device:TPU:0 before, /device:TPU:24 now
where the time goes in v2:
time: 46.2 us; the launch traced here: 45.9 us
  Pallas kernels  42.9 us (93%)
  local copies, waits for them, and re-layouts  2.33 us (5%)
  between operations  0.65 us (1%)
    pallas_call x1, Pallas kernels, fused_body(): pl.pallas_call(functools.partial(kernel, depth, width), out_shape=(whole,...  42.9 us
    unnamed x4, local copies, waits for them, and re-layouts  2.33 us

profile of v2, /device:TPU:24, one launch (start us, length us, event | category | flops | bytes accessed | tf_op | source)
XLA Modules:
  0.0 45.9 jit_solution(12546859116949933498)
XLA Ops:
  0.6 0.0 copy-start
  0.6 0.7 %copy-done = s32[2304]{0:T(1024)S(1)} copy-done((s32[2304]{0:T(1024)S(1)}, s32[2304]{0:T(1024)}, u32[]{:S(2)}) %copy-start) | copy-done | bytes 9240
  1.3 42.9 %shard_map.59 = (f32[64,2304]{1,0:T(8,128)S(1)}, f32[64,2304]{1,0:T(8,128)S(1)}) custom-call(f32[1152,2304]{1,0:T(8,128)} %a_ref.1, f32[18,128,128]{2,1,0:T(8,128)} %tile_ref.1, f32[64,2304]{1,0:T(8,128)} %bitcast.7, s32[18,128]{1,0:T(8,128)S(1)} %bitcast.6), custom_call_target="tpu_custom_call" | custom-call | tf_op jit(solution)/shard_map/pallas_call | solution.py:553
  44.3 0.8 %copy.8 = f32[2304,64]{0,1:T(8,128)} copy(f32[2304,64]{0,1:T(8,128)S(1)} %bitcast.5) | data formatting | bytes 1179648
  45.1 0.8 %copy.9 = f32[2304,64]{0,1:T(8,128)} copy(f32[2304,64]{0,1:T(8,128)S(1)} %bitcast.4) | data formatting | bytes 1179648
Async XLA Ops:
  0.6 0.7 %copy-start = (s32[2304]{0:T(1024)S(1)}, s32[2304]{0:T(1024)}, u32[]{:S(2)}) copy-start(s32[2304]{0:T(1024)} %param.7) | copy-start | bytes 27652

commit v3 on v2

--- a/solution.py
+++ b/solution.py
@@ -9,7 +9,8 @@
 
 ITERS = 2
 MESH = pl.DeviceIdType.MESH
-NEAR_LAG = 3
+NEAR_LAG = 2
+FETCHES = ((0, 1), (1, 2), (3, 2), (5, 2), (7, 2))
 
 
 def masked_tiles(tile_inverse, order_ids):
@@ -113,10 +114,10 @@
     a_ref, tile_ref, b_ref, ids_ref,
     sol_ref, res_ref,
     a_buf, a_split, tile_buf, tile_split, v_split, v_minus, m_split, b_buf, u_buf, m_buf,
-    part, near, half, far, done, image, acc,
+    part, near, half, far, done, hop, image, acc,
     sums, dot_own, dot_in, delta_own, delta_fill, delta_in, ids_buf,
-    a_sem, in_sem, near_sem, far_sem, line_sem, side_sem,
-    near_send, far_send, fan_send, relay_send, dot_send, dot_recv, delta_send, delta_recv,
+    a_sem, in_sem, near_sem, far_sem, line_sem, side_sem, hop_sem,
+    near_send, far_send, hop_send, slant_send, fan_send, relay_send, dot_send, dot_recv, delta_send, delta_recv,
 ):
     my_row, my_col = lax.axis_index("row"), lax.axis_index("col")
     place, lane = my_row // 2, lax.rem(my_row, 2)
@@ -137,8 +138,12 @@
     mine = pl.ds(pl.multiple_of(core * hh, hh), hh)
     other = pl.ds(pl.multiple_of((1 - core) * hh, hh), hh)
 
-    def fetch(i):
-        return pltpu.make_async_copy(a_ref.at[pl.ds(i * width, width)], a_buf.at[i], a_sem.at[i])
+    def fetch(k):
+        begin, count = FETCHES[k]
+        return pltpu.make_async_copy(
+            a_ref.at[pl.ds(begin * width, count * width)],
+            a_buf.at[pl.ds(begin * width, count * width)], a_sem.at[k],
+        )
 
     first_tiles = tiles // 2
     pieces = (pl.ds(0, first_tiles), pl.ds(first_tiles, tiles - first_tiles))
@@ -159,17 +164,21 @@
     for shift in range(1, 4):
         greet(my_row, lax.rem(my_col + shift, 4))
     greet(side, my_col)
-    greet(2 * my_col + 1 - lane, my_col)
-
-    @pl.when(others)
-    def _():
-        greet(2 * my_col + lane, my_col)
-
-    @pl.when(place > my_col)
+
+    last = depth - 1
+    at_end = jnp.logical_or(place == 0, place == last)
+    carrier = jnp.logical_and(at_end, owner_chip)
+    origin = jnp.logical_and(at_end, jnp.logical_not(owner_chip))
+    far_end = 2 * (last - place) + lane
+    carried = jnp.logical_and(at_end, my_col == last - place)
+    from_line = jnp.logical_and(others, jnp.logical_not(carried))
+    slanted = jnp.logical_and(carrier, core == 0)
+
+    @pl.when(jnp.logical_and(from_line, place > my_col))
     def _():
         greet(my_row - 2, my_col)
 
-    @pl.when(place < my_col)
+    @pl.when(jnp.logical_and(from_line, place < my_col))
     def _():
         greet(my_row + 2, my_col)
 
@@ -181,8 +190,16 @@
     def _():
         greet(side, partner)
 
-    goes_up = jnp.logical_and(place >= my_col, above)
-    goes_down = jnp.logical_and(place <= my_col, below)
+    @pl.when(carrier)
+    def _():
+        greet(far_end, my_col)
+
+    @pl.when(carried)
+    def _():
+        greet(side, 2 * (place // 2))
+
+    goes_up = jnp.logical_and(jnp.logical_and(place >= my_col, above), my_col + last - 1 != place)
+    goes_down = jnp.logical_and(jnp.logical_and(place <= my_col, below), my_col - last + 1 != place)
 
     def one(flag):
         return jnp.where(flag, 1, 0)
@@ -190,7 +207,7 @@
     def meet():
         awaited = 4 + one(goes_up) + one(goes_down)
         awaited += jnp.where(helper, 1 + one(above) + one(below), 0)
-        awaited += jnp.where(owner, 2 * depth - 1, 0)
+        awaited += one(origin) + one(slanted)
         pl.semaphore_wait(barrier, awaited)
 
     def lanes_at(t):
@@ -202,10 +219,12 @@
     def lanes_of(block, q):
         return lanes_at(block * steps + q)
 
-    def near_chunk(turn, q):
-        return pltpu.make_async_remote_copy(
-            src_ref=part.at[turn, other, cut(q)], dst_ref=near.at[turn, :, cut(q)],
-            send_sem=near_send.at[turn], recv_sem=near_sem.at[turn, q],
+    def near_group(turn, k):
+        begin, count = FETCHES[k]
+        lanes = pl.ds(begin * width, count * width)
+        return pltpu.make_async_remote_copy(
+            src_ref=part.at[turn, other, lanes], dst_ref=near.at[turn, :, lanes],
+            send_sem=near_send.at[turn], recv_sem=near_sem.at[turn, k],
             device_id=(my_row, partner), device_id_type=MESH,
         )
 
@@ -230,21 +249,71 @@
             device_id=(row, my_col), device_id_type=MESH,
         )
 
-    def stage1(turn, q):
-        near_chunk(turn, q).wait_recv()
-        half[turn, :, cut(q)] = part[turn, mine, cut(q)] + near[turn, :, cut(q)]
-
-        @pl.when(jnp.logical_not(owner_chip))
-        def _():
-            far_chunk(turn, q).start()
+    def hop_chunk(turn, q):
+        return pltpu.make_async_remote_copy(
+            src_ref=done.at[turn, :, cut(q)], dst_ref=hop.at[turn, :, cut(q)],
+            send_sem=hop_send.at[turn], recv_sem=hop_sem.at[turn, q],
+            device_id=(far_end, my_col), device_id_type=MESH,
+        )
+
+    def cross_chunk(turn, q):
+        return pltpu.make_async_remote_copy(
+            src_ref=hop.at[turn, :, cut(q)], dst_ref=image.at[turn, mine, lanes_of(lane, q)],
+            send_sem=hop_send.at[turn], recv_sem=line_sem.at[turn, q],
+            device_id=(my_row, last - place), device_id_type=MESH,
+        )
+
+    def slant_chunk(turn, q):
+        return pltpu.make_async_remote_copy(
+            src_ref=hop.at[turn, :, cut(q)], dst_ref=image.at[turn, mine, lanes_of(lane, q)],
+            send_sem=slant_send.at[turn], recv_sem=side_sem.at[turn, q],
+            device_id=(side, last - place), device_id_type=MESH,
+        )
+
+    def half_chunk(turn, q):
+        rows_lanes = (turn, pl.ds(hh, hh), lanes_of(lane, q))
+        return pltpu.make_async_remote_copy(
+            src_ref=image.at[rows_lanes], dst_ref=image.at[rows_lanes],
+            send_sem=relay_send.at[turn, 1], recv_sem=side_sem.at[turn, q],
+            device_id=(side, my_col), device_id_type=MESH,
+        )
+
+    sends_far = jnp.logical_or(at_end, jnp.logical_not(owner_chip))
+    takes_far = jnp.logical_or(at_end, owner_chip)
+
+    def stage1(turn, k):
+        near_group(turn, k).wait_recv()
+        begin, count = FETCHES[k]
+        for q in range(begin, begin + count):
+            half[turn, :, cut(q)] = part[turn, mine, cut(q)] + near[turn, :, cut(q)]
+
+        @pl.when(sends_far)
+        def _():
+            for q in range(begin, begin + count):
+                far_chunk(turn, q).start()
+
+    def carry(turn, q):
+        @pl.when(carrier)
+        def _():
+            hop_chunk(turn, q).wait_recv()
+            cross_chunk(turn, q).start()
+
+            @pl.when(core == 0)
+            def _():
+                slant_chunk(turn, q).start()
 
     def stage2(turn, q):
+        @pl.when(takes_far)
+        def _():
+            far_chunk(turn, q).wait_recv()
+            done[turn, :, cut(q)] = half[turn, :, cut(q)] + far[turn, :, cut(q)]
+
+        @pl.when(origin)
+        def _():
+            hop_chunk(turn, q).start()
+
         @pl.when(owner_chip)
         def _():
-            far_chunk(turn, q).wait_recv()
-            total = half[turn, :, cut(q)] + far[turn, :, cut(q)]
-            done[turn, :, cut(q)] = total
-
             @pl.when(above)
             def _():
                 fan_chunk(turn, q, 0, my_row + 2, line_sem).start()
@@ -261,7 +330,7 @@
 
             @pl.when(owner)
             def _():
-                image[turn, mine, lanes_of(lane, q)] = total
+                image[turn, mine, lanes_of(lane, q)] = done[turn, :, cut(q)]
 
     def own(turn, q):
         @pl.when(owner)
@@ -284,7 +353,13 @@
             def _():
                 relay_chunk(turn, q, 0, my_row - 2, line_sem).start()
 
-            relay_chunk(turn, q, 1, side, side_sem).start()
+            @pl.when(from_line)
+            def _():
+                relay_chunk(turn, q, 1, side, side_sem).start()
+
+            @pl.when(carried)
+            def _():
+                half_chunk(turn, q).start()
 
     def beside(turn, q):
         pltpu.make_async_remote_copy(
@@ -315,7 +390,15 @@
                 device_id=(side, my_col), device_id_type=MESH,
             )
 
-        @pl.when(jnp.logical_not(owner_chip))
+        @pl.when(at_end)
+        def _():
+            pltpu.make_async_remote_copy(
+                src_ref=hop.at[turn], dst_ref=hop.at[turn],
+                send_sem=hop_send.at[turn], recv_sem=hop_sem.at[turn, 0],
+                device_id=(far_end, my_col), device_id_type=MESH,
+            ).wait_send()
+
+        @pl.when(sends_far)
         def _():
             pltpu.make_async_remote_copy(
                 src_ref=half.at[turn], dst_ref=far.at[turn],
@@ -345,7 +428,25 @@
             def _():
                 relay_all(0).wait_send()
 
-            relay_all(1).wait_send()
+            @pl.when(from_line)
+            def _():
+                relay_all(1).wait_send()
+
+        @pl.when(carried)
+        def _():
+            pltpu.make_async_remote_copy(
+                src_ref=half.at[turn], dst_ref=half.at[turn],
+                send_sem=relay_send.at[turn, 1], recv_sem=side_sem.at[turn, 0],
+                device_id=(side, my_col), device_id_type=MESH,
+            ).wait_send()
+
+        @pl.when(slanted)
+        def _():
+            pltpu.make_async_remote_copy(
+                src_ref=hop.at[turn], dst_ref=hop.at[turn],
+                send_sem=slant_send.at[turn], recv_sem=hop_sem.at[turn, 0],
+                device_id=(side, my_col), device_id_type=MESH,
+            ).wait_send()
 
     def dot_row():
         return jnp.sum(sums[...].T, axis=0, keepdims=True)
@@ -375,12 +476,11 @@
     fetch(0).start()
     fetch_tiles(0).wait()
     fetch(1).start()
-    fetch(2).start()
     for t in range(tiles):
         if t == first_tiles:
             fetch_tiles(1).wait()
             fetch_b.wait()
-            for i in range(3, steps):
+            for i in range(2, len(FETCHES)):
                 fetch(i).start()
         same = ids_across[:, t : t + 1] == ids_buf[t : t + 1]
         tile_split[t] = jnp.concatenate(halves(jnp.where(same, tile_buf[t], 0.0)), axis=1)
@@ -396,27 +496,20 @@
     sums[:nrhs] = gamma
     sums[nrhs:] = jnp.zeros_like(gamma)
 
-    met = False
-    halved = 0
-    for begin in [0] + list(range(1, steps, 2)):
-        group = range(begin, min(begin + 2, steps)) if begin else range(1)
-        for q in group:
-            fetch(q).wait()
-        for q in group:
-            a_split[q] = split(a_buf[q])
+    for k, (begin, count) in enumerate(FETCHES):
+        fetch(k).wait()
+        for q in range(begin, begin + count):
+            a_split[q] = split(a_buf[q * width : (q + 1) * width])
             high = times_transposed(v_split[...], a_split[q, :width])
             minus_low = times_transposed(v_minus[...], a_split[q, width:])
             part[0, :, cut(q)] = (high[:nrhs] - minus_low[:nrhs]) + (high[nrhs:] - minus_low[nrhs:])
-        if not met:
+        if k == 0:
             meet()
-            met = True
-        for q in group:
-            near_chunk(0, q).start()
-        while halved <= group[-1] - NEAR_LAG:
-            stage1(0, halved)
-            halved += 1
-    for q in range(halved, steps):
-        stage1(0, q)
+        near_group(0, k).start()
+        if k >= NEAR_LAG:
+            stage1(0, k - NEAR_LAG)
+    for k in range(len(FETCHES) - NEAR_LAG, len(FETCHES)):
+        stage1(0, k)
 
     acc[...] = jnp.zeros_like(acc)
 
@@ -439,6 +532,8 @@
     for q in range(steps):
         stage2(0, q)
     arrivals = [(lane, q) for q in range(steps)] + [(1 - lane, q) for q in range(steps)]
+    for q in range(steps):
+        carry(0, q)
     taken = []
     for begin in range(0, 2 * steps, 2):
         for k in (begin, begin + 1):
@@ -452,11 +547,11 @@
         taken = [take(*arrivals[k], k % 4) for k in (begin, begin + 1)]
     for i in range(steps):
         part[1, :, cut(i)] = update(taken, i)
-    for i in range(steps):
-        near_chunk(1, i).start()
+    for k in range(len(FETCHES)):
+        near_group(1, k).start()
     exchange(0, dot_row())
-    for q in range(steps):
-        stage1(1, q)
+    for k in range(len(FETCHES)):
+        stage1(1, k)
     gamma0, delta0 = exchanged(0)
     alpha0 = gamma0 / delta0
     gamma = jnp.zeros((nrhs, width), jnp.float32)
@@ -492,6 +587,7 @@
     for q in range(steps):
         stage2(1, q)
     for q in range(steps):
+        carry(1, q)
         own(1, q)
 
         @pl.when(owner)
@@ -556,7 +652,7 @@
         in_specs=[hbm, hbm, hbm, vmem],
         out_specs=(vmem, vmem),
         scratch_shapes=[
-            pltpu.VMEM((steps, width, block_cols), f32),
+            pltpu.VMEM((block_rows, block_cols), f32),
             pltpu.VMEM((steps, 2 * width, block_cols), bf16),
             pltpu.VMEM((tiles, width, width), f32),
             pltpu.VMEM((tiles, width, 2 * width), bf16),
@@ -571,6 +667,7 @@
             pltpu.VMEM((2, hh, block_rows), f32),
             pltpu.VMEM((2, hh, block_rows), f32),
             pltpu.VMEM((2, hh, block_rows), f32),
+            pltpu.VMEM((2, hh, block_rows), f32),
             pltpu.VMEM((2, nrhs, block_cols), f32),
             pltpu.VMEM((nrhs, block_rows), f32),
             pltpu.VMEM((2 * nrhs, width), f32),
@@ -580,12 +677,15 @@
             pltpu.VMEM((8 * depth - 1, 8, width), f32),
             pltpu.VMEM((2 * depth, 8, width), f32),
             pltpu.VMEM((width, width), f32),
-            dma((steps,)),
+            dma((len(FETCHES),)),
             dma((3,)),
+            dma((2, len(FETCHES))),
             dma((2, steps)),
             dma((2, steps)),
             dma((2, steps)),
             dma((2, steps)),
+            dma((2,)),
+            dma((2,)),
             dma((2,)),
             dma((2,)),
             dma((2, 4)),
@@ -611,6 +711,7 @@
         and block_cols == 2 * block_rows
         and block_rows % width == 0
         and width == 128
+        and block_rows == width * (FETCHES[-1][0] + FETCHES[-1][1])
         and tile_inverse.shape[0] <= width
         and right_side.shape[1] == 64
     )

time: 46.2 us -> 43.2 us (0.935)
  the two profiles are of different devices: /device:TPU:24 before, /device:TPU:16 now
where the time goes in v3:
time: 43.2 us; the launch traced here: 42.8 us
  Pallas kernels  39.9 us (92%)
  local copies, waits for them, and re-layouts  2.33 us (5%)
  between operations  0.65 us (2%)
    pallas_call x1, Pallas kernels, fused_body(): pl.pallas_call(functools.partial(kernel, depth, width), out_shape=(whole,...  39.9 us
    unnamed x4, local copies, waits for them, and re-layouts  2.33 us

profile of v3, /device:TPU:16, one launch (start us, length us, event | category | flops | bytes accessed | tf_op | source)
XLA Modules:
  0.0 42.8 jit_solution(3929342529059247849)
XLA Ops:
  0.6 0.0 copy-start
  0.6 0.7 %copy-done = s32[2304]{0:T(1024)S(1)} copy-done((s32[2304]{0:T(1024)S(1)}, s32[2304]{0:T(1024)}, u32[]{:S(2)}) %copy-start) | copy-done | bytes 9240
  1.3 39.9 %shard_map.59 = (f32[64,2304]{1,0:T(8,128)S(1)}, f32[64,2304]{1,0:T(8,128)S(1)}) custom-call(f32[1152,2304]{1,0:T(8,128)} %a_ref.1, f32[18,128,128]{2,1,0:T(8,128)} %tile_ref.1, f32[64,2304]{1,0:T(8,128)} %bitcast.7, s32[18,128]{1,0:T(8,128)S(1)} %bitcast.6), custom_call_target="tpu_custom_call" | custom-call | tf_op jit(solution)/shard_map/pallas_call | solution.py:649
  41.2 0.8 %copy.8 = f32[2304,64]{0,1:T(8,128)} copy(f32[2304,64]{0,1:T(8,128)S(1)} %bitcast.5) | data formatting | bytes 1179648
  42.0 0.8 %copy.9 = f32[2304,64]{0,1:T(8,128)} copy(f32[2304,64]{0,1:T(8,128)S(1)} %bitcast.4) | data formatting | bytes 1179648
Async XLA Ops:
  0.6 0.7 %copy-start = (s32[2304]{0:T(1024)S(1)}, s32[2304]{0:T(1024)}, u32[]{:S(2)}) copy-start(s32[2304]{0:T(1024)} %param.7) | copy-start | bytes 27652
